TPU v7x, 32 devices: a whole 2x2x4 slice. The times are simulated.
32 devices in a mesh: grp: 2 (over y), gx: 16 (over z, x, core), gy: 1.
Axes of the slice: x: 2, y: 2, z: 4, core: 2. Of those that a mesh axis runs over, the one named last changes fastest.
Arguments:
- residue_feats: bfloat16 [512, 256], P(('grp', 'gx')), parts along dimension 0, may hold values from -6 to 6
- pair_feats: bfloat16 [64, 512, 256], P(None, ('grp', 'gx'), 'gy'), parts along dimension 1, may hold values from -30 to 30
- w_row: bfloat16 [256, 64], replicated, may hold values from -0.375 to 0.375
- w_col: bfloat16 [256, 64], replicated, may hold values from -0.375 to 0.375
- first_taps: bfloat16 [9, 64, 64], replicated, may hold values from -0.25 to 0.25
- second_taps: bfloat16 [9, 64, 64], replicated, may hold values from -0.25 to 0.25
- norm_scale: float32 [2, 64], replicated, may hold values from 0.25 to 1.75
- norm_shift: float32 [2, 64], replicated, may hold values from -2 to 2
Outputs:
- symmetric: bfloat16 [64, 512, 256], P(None, ('grp', 'gx'), 'gy'), parts along dimension 1
There are 2 independent parts, one for each index of `grp`. A program takes and returns all parts, laid end to end along the dimension named above; an argument that names none is the same for every part. Nothing has to cross between parts.
All inputs are finite; a program needn't handle non-finite values.
Results may differ from a plain program's by a relative error of at most 0.012.
Values may be sent and summed in bfloat16 or wider, within the bound.
A program may use at most 64 MiB of HBM per device.

v0:
```python
import jax
import jax.numpy as jnp
from jax import lax
from jax.sharding import PartitionSpec as P

DILATION_STEP = 8


epsilon = 1e-05


def with_halo(cells, sides, width):
    for axis, dim in sides:
        count = lax.axis_size(axis)
        ends = count - 1
        head = lax.slice_in_dim(cells, 0, width, axis=dim)
        tail = lax.slice_in_dim(cells, cells.shape[dim] - width, cells.shape[dim], axis=dim)
        cells = jnp.concatenate(
            [
                lax.ppermute(tail, axis, [(i, (i + 1) % count) for i in range(ends)]),
                cells,
                lax.ppermute(head, axis, [((i + 1) % count, i) for i in range(ends)]),
            ],
            axis=dim,
        )
    return cells


def dilated(receptive_region, weights):
    row_count = receptive_region.shape[1]
    col_count = receptive_region.shape[2]
    border_padded_input = with_halo(receptive_region, (("gx", 1), ("gy", 2)), DILATION_STEP)
    tap_sum_total = jnp.zeros((weights.shape[1], row_count, col_count), jnp.float32)
    for filter_tap_index in range(9):
        row_displacement = filter_tap_index // 3 * DILATION_STEP
        column_displacement = filter_tap_index % 3 * DILATION_STEP
        window = border_padded_input[
            :,
            row_displacement : row_displacement + row_count,
            column_displacement : column_displacement + col_count,
        ]
        tap_sum_total = tap_sum_total + jnp.einsum(
            "oc,crw->orw", weights[filter_tap_index], window, preferred_element_type=jnp.float32
        )
    return tap_sum_total


def normalized(tap_sum_total, gain, shift):
    cell_count = (
        tap_sum_total.shape[1] * tap_sum_total.shape[2] * lax.axis_size("gx") * lax.axis_size("gy")
    )
    first_sum, second_sum = lax.psum(
        (jnp.sum(tap_sum_total, axis=(1, 2)), jnp.sum(tap_sum_total * tap_sum_total, axis=(1, 2))),
        ("gx", "gy"),
    )
    average = first_sum / cell_count
    spread = second_sum / cell_count - average * average
    centred = tap_sum_total - average[:, None, None]
    factor = gain * lax.rsqrt(spread + epsilon)
    return centred * factor[:, None, None] + shift[:, None, None]


def body(residue_feats, pair_feats, w_row, w_col, first_taps, second_taps, norm_scale, norm_shift):
    col_count = pair_feats.shape[2]
    col_start = lax.axis_index("gy") * col_count
    row_part = jnp.dot(residue_feats, w_row, preferred_element_type=jnp.float32).astype(
        jnp.bfloat16
    )
    everyone = lax.all_gather(residue_feats, "gx", axis=0, tiled=True)
    col_feats = lax.dynamic_slice_in_dim(everyone, col_start, col_count, 0)
    col_part = jnp.dot(col_feats, w_col, preferred_element_type=jnp.float32).astype(jnp.bfloat16)
    block_in = (
        pair_feats.astype(jnp.float32)
        + row_part.T.astype(jnp.float32)[:, :, None]
        + col_part.T.astype(jnp.float32)[:, None, :]
    ).astype(jnp.bfloat16)
    first_conv = dilated(block_in, first_taps)
    activated = jax.nn.elu(normalized(first_conv, norm_scale[0], norm_shift[0])).astype(
        jnp.bfloat16
    )
    second_conv = dilated(activated, second_taps)
    block_out = jax.nn.elu(
        block_in.astype(jnp.float32) + normalized(second_conv, norm_scale[1], norm_shift[1])
    ).astype(jnp.bfloat16)
    whole_rows = lax.all_gather(block_out, "gy", axis=2, tiled=True)
    columns = lax.all_to_all(whole_rows, "gx", split_axis=2, concat_axis=1, tiled=True)
    flipped = lax.dynamic_slice_in_dim(columns, col_start, col_count, 1)
    mirrored = jnp.transpose(flipped, (0, 2, 1))
    return (0.5 * (block_out.astype(jnp.float32) + mirrored.astype(jnp.float32))).astype(
        jnp.bfloat16
    )


def solution(mesh):
    placed = (P(("grp", "gx"), None), P(None, ("grp", "gx"), "gy"), P(), P(), P(), P(), P(), P())
    return jax.shard_map(
        body, mesh=mesh, in_specs=placed, out_specs=P(None, ("grp", "gx"), "gy"), check_vma=False
    )
```

profile of v0, /device:TPU:0, one launch (start us, length us, event | category | flops | bytes accessed | tf_op | source)
XLA Modules:
  0.0 140.1 jit_solution(18333366935052121485)
XLA Ops:
  0.0 0.0 copy-start
  0.0 23.8 %all_gather.4 = bf16[256,256]{1,0:T(8,128)(2,1)S(1)} all-gather(bf16[16,256]{1,0:T(8,128)(2,1)} %param.8), channel_id=1, replica_groups=mesh['grp'=2,'gx'=16,'gy'=1] {'gx'}, dimensions={0}, use_global_device_ids=true | all-gather | bytes 139264 | tf_op jit(solution)/shard_map/all_gather | solution.py:69
  23.8 0.9 fusion.13
  24.7 0.0 copy-done
  24.7 0.2 fusion.12
  24.9 1.3 add_convert_fusion
  26.2 2.3 %collective-permute-start = (bf16[64,8,256]{2,0,1:T(8,128)(2,1)S(1)}, bf16[64,8,256]{2,0,1:T(8,128)(2,1)S(1)}, u32[]{:S(2)}, u32[]{:S(2)}) collective-permute-start(bf16[64,8,256]{2,0,1:T(8,128)(2,1)S(1)} %get-tuple-element.23), channel_id=1, source_target_pairs={{0,1},{1,2},{2,3},{3,4},{4,5},{5,6},{6,7},{7,8},{8,9},{9,10},{10,1... | collective-permute-start | bytes 786440 | tf_op jit(solution)/shard_map/ppermute | solution.py:20
  28.5 1.3 collective-permute-start.1
  29.8 0.3 fusion.62
  30.1 0.0 collective-permute-done
  30.1 1.8 %collective-permute-done.1 = bf16[64,8,256]{2,0,1:T(8,128)(2,1)S(1)} collective-permute-done((bf16[64,8,256]{2,0,1:T(8,128)(2,1)S(1)}, bf16[64,8,256]{2,0,1:T(8,128)(2,1)S(1)}, u32[]{:S(2)}, u32[]{:S(2)}) %collective-permute-start.1) | collective-permute-done | bytes 262176 | tf_op jit(solution)/shard_map/ppermute | solution.py:22
  31.9 0.1 pad_maximum_fusion.2
  32.1 0.3 fusion.93
  32.3 0.7 collective-permute-start.2
  33.0 0.7 collective-permute-start.3
  33.7 0.3 fusion.45
  34.0 0.3 fusion.36
  34.3 0.0 collective-permute-done.2
  34.3 0.0 collective-permute-done.3
  34.3 1.3 maximum_maximum_fusion
  35.6 0.4 fusion.43
  36.0 0.4 fusion.34
  36.4 0.3 fusion.41
  36.7 0.3 fusion.38
  36.9 0.4 fusion.11
  37.3 0.0 copy-start.4
  37.3 0.7 fusion.91
  38.0 0.0 copy-start.3
  38.0 33.9 %all-reduce.1 = (f32[64]{0:T(128)S(1)}, f32[64]{0:T(128)S(1)}) all-reduce(f32[64]{0:T(128)S(1)} %get-tuple-element.8, f32[64]{0:T(128)S(1)} %get-tuple-element.7), channel_id=1, replica_groups=mesh['grp'=2,'gx'=16,'gy'=1] {'gx','gy'}, use_global_device_ids=true, to_apply=%region_3.0 | all-reduce | flops 128 | bytes 1024 | tf_op jit(solution)/shard_map/psum | solution.py:52
  72.0 0.6 fusion.15
  72.6 1.3 collective-permute-start.4
  73.9 1.3 collective-permute-start.5
  75.2 0.3 fusion.52
  75.5 0.0 collective-permute-done.4
  75.5 1.8 %collective-permute-done.5 = bf16[64,8,256]{2,0,1:T(8,128)(2,1)S(1)} collective-permute-done((bf16[64,8,256]{2,0,1:T(8,128)(2,1)S(1)}, bf16[64,8,256]{2,0,1:T(8,128)(2,1)S(1)}, u32[]{:S(2)}, u32[]{:S(2)}) %collective-permute-start.5) | collective-permute-done | bytes 262176 | tf_op jit(solution)/shard_map/ppermute | solution.py:22
  77.4 0.1 pad_maximum_fusion.3
  77.5 0.3 fusion.92
  77.8 0.7 collective-permute-start.6
  78.5 0.7 collective-permute-start.7
  79.2 0.3 fusion.31
  79.4 0.3 fusion.22
  79.7 0.0 collective-permute-done.6
  79.7 0.0 collective-permute-done.7
  79.7 1.3 maximum_maximum_fusion.1
  81.0 0.4 fusion.29
  81.4 0.4 fusion.20
  81.8 0.3 fusion.27
  82.1 0.3 fusion.24
  82.3 0.4 fusion.5
  82.7 0.0 copy-start.1
  82.8 0.7 fusion.90
  83.4 31.5 %all-reduce = (f32[64]{0:T(128)S(1)}, f32[64]{0:T(128)S(1)}) all-reduce(f32[64]{0:T(128)S(1)} %get-tuple-element.6, f32[64]{0:T(128)S(1)} %get-tuple-element.5), channel_id=1, replica_groups=mesh['grp'=2,'gx'=16,'gy'=1] {'gx','gy'}, use_global_device_ids=true, to_apply=%region_7.8 | all-reduce | flops 128 | bytes 1024 | tf_op jit(solution)/shard_map/psum | solution.py:52
  115.0 0.0 copy-done.1
  115.0 0.7 fusion.17
  115.7 1.0 copy.18
  116.7 0.7 reshape.32
  117.4 16.9 %all_to_all.4 = bf16[16,2,8192]{2,1,0:T(2,128)(2,1)S(1)} all-to-all(bf16[16,2,8192]{2,1,0:T(2,128)(2,1)S(1)} %reshape.32), channel_id=1, replica_groups=mesh['grp'=2,'gx'=16,'gy'=1] {'gx'}, dimensions={0} | all-to-all | bytes 1048576 | tf_op jit(solution)/shard_map/all_to_all | solution.py:86
  134.3 0.7 reshape.33
  135.0 0.3 copy.19
  135.2 0.2 convert_bitcast_fusion
  135.5 0.2 copy.20
  135.7 2.0 %copy.21 = f32[64,256,16]{1,0,2:T(8,128)} copy(f32[64,256,16]{0,2,1:T(8,128)S(1)} %bitcast.109) | data formatting | bytes 2097152 | tf_op jit(solution)/shard_map/convert_element_type | solution.py:89
  137.6 1.4 fusion.19
  139.0 1.1 copy.22
  (11 shorter events, 0.1 us)
Async XLA Ops:
  0.0 24.7 %copy-start = (bf16[256,64]{0,1:T(8,128)(2,1)S(1)}, bf16[256,64]{0,1:T(8,128)(2,1)}, u32[]{:S(2)}) copy-start(bf16[256,64]{0,1:T(8,128)(2,1)} %param.11) | copy-start | bytes 98308
  0.0 29.8 %copy-start.5 = (f32[2,64]{1,0:T(2,128)S(1)}, f32[2,64]{1,0:T(2,128)}, u32[]{:S(2)}) copy-start(f32[2,64]{1,0:T(2,128)} %param.15) | copy-start | bytes 1540
  0.0 29.8 %copy-start.2 = (bf16[9,64,64]{2,1,0:T(8,128)(2,1)S(1)}, bf16[9,64,64]{2,1,0:T(8,128)(2,1)}, u32[]{:S(2)}) copy-start(bf16[9,64,64]{2,1,0:T(8,128)(2,1)} %param.12) | copy-start | bytes 221188
  26.2 3.9 %collective-permute-start = (bf16[64,8,256]{2,0,1:T(8,128)(2,1)S(1)}, bf16[64,8,256]{2,0,1:T(8,128)(2,1)S(1)}, u32[]{:S(2)}, u32[]{:S(2)}) collective-permute-start(bf16[64,8,256]{2,0,1:T(8,128)(2,1)S(1)} %get-tuple-element.23), channel_id=1, source_target_pairs={{0,1},{1,2},{2,3},{3,4},{4,5},{5,6},{6,7},{7,8},{8,9},{9,10},{10,1... | collective-permute-start | bytes 786440 | tf_op jit(solution)/shard_map/ppermute | solution.py:20
  28.5 3.4 %collective-permute-start.1 = (bf16[64,8,256]{2,0,1:T(8,128)(2,1)S(1)}, bf16[64,8,256]{2,0,1:T(8,128)(2,1)S(1)}, u32[]{:S(2)}, u32[]{:S(2)}) collective-permute-start(bf16[64,8,256]{2,0,1:T(8,128)(2,1)S(1)} %get-tuple-element.24), channel_id=1, source_target_pairs={{1,0},{2,1},{3,2},{4,3},{5,4},{6,5},{7,6},{8,7},{9,8},{10,9},{11,1... | collective-permute-start | bytes 786440 | tf_op jit(solution)/shard_map/ppermute | solution.py:22
  32.3 1.9 %collective-permute-start.2 = (bf16[64,32,8]{2,0,1:T(8,128)(2,1)S(1)}, bf16[64,32,8]{2,0,1:T(8,128)(2,1)S(1)}, u32[]{:S(2)}, u32[]{:S(2)}) collective-permute-start(bf16[64,32,8]{2,0,1:T(8,128)(2,1)S(1)} %get-tuple-element.19), channel_id=1, source_target_pairs={} | collective-permute-start | bytes 98312 | tf_op jit(solution)/shard_map/ppermute | solution.py:20
  33.0 1.3 collective-permute-start.3
  37.3 34.6 %copy-start.4 = (f32[2,64]{1,0:T(2,128)S(1)}, f32[2,64]{1,0:T(2,128)}, u32[]{:S(2)}) copy-start(f32[2,64]{1,0:T(2,128)} %param.14) | copy-start | bytes 1540
  38.0 37.2 %copy-start.3 = (bf16[9,64,64]{2,1,0:T(8,128)(2,1)S(1)}, bf16[9,64,64]{2,1,0:T(8,128)(2,1)}, u32[]{:S(2)}) copy-start(bf16[9,64,64]{2,1,0:T(8,128)(2,1)} %param.13) | copy-start | bytes 221188
  72.6 2.9 %collective-permute-start.4 = (bf16[64,8,256]{2,0,1:T(8,128)(2,1)S(1)}, bf16[64,8,256]{2,0,1:T(8,128)(2,1)S(1)}, u32[]{:S(2)}, u32[]{:S(2)}) collective-permute-start(bf16[64,8,256]{2,0,1:T(8,128)(2,1)S(1)} %get-tuple-element.21), channel_id=1, source_target_pairs={{0,1},{1,2},{2,3},{3,4},{4,5},{5,6},{6,7},{7,8},{8,9},{9,10},{10,1... | collective-permute-start | bytes 786440 | tf_op jit(solution)/shard_map/ppermute | solution.py:20
  73.9 3.4 %collective-permute-start.5 = (bf16[64,8,256]{2,0,1:T(8,128)(2,1)S(1)}, bf16[64,8,256]{2,0,1:T(8,128)(2,1)S(1)}, u32[]{:S(2)}, u32[]{:S(2)}) collective-permute-start(bf16[64,8,256]{2,0,1:T(8,128)(2,1)S(1)} %get-tuple-element.22), channel_id=1, source_target_pairs={{1,0},{2,1},{3,2},{4,3},{5,4},{6,5},{7,6},{8,7},{9,8},{10,9},{11,1... | collective-permute-start | bytes 786440 | tf_op jit(solution)/shard_map/ppermute | solution.py:22
  77.8 1.9 %collective-permute-start.6 = (bf16[64,32,8]{2,0,1:T(8,128)(2,1)S(1)}, bf16[64,32,8]{2,0,1:T(8,128)(2,1)S(1)}, u32[]{:S(2)}, u32[]{:S(2)}) collective-permute-start(bf16[64,32,8]{2,0,1:T(8,128)(2,1)S(1)} %get-tuple-element.15), channel_id=1, source_target_pairs={} | collective-permute-start | bytes 98312 | tf_op jit(solution)/shard_map/ppermute | solution.py:20
  78.5 1.3 collective-permute-start.7
  82.7 32.2 %copy-start.1 = (bf16[64,16,256]{2,1,0:T(8,128)(2,1)S(1)}, bf16[64,16,256]{2,1,0:T(8,128)(2,1)}, u32[]{:S(2)}) copy-start(bf16[64,16,256]{2,1,0:T(8,128)(2,1)} %param.9) | copy-start | bytes 1572868
where the time goes:
time: 141 us; the launch traced here: 140 us
  blocking collectives  106 us (75%)
  starting transfers between devices  8.9 us (6%)
  matrix products  7.38 us (5%)
  other arithmetic  7.08 us (5%)
  local copies, waits for them, and re-layouts  6.52 us (5%)
  waiting for transfers between devices  3.66 us (3%)
    psum x2, blocking collectives, normalized(): lax.psum((jnp.sum(tap_sum_total, axis=(1, 2)), jnp.sum(tap_sum_total * ta...  65.5 us
    all_gather x1, blocking collectives, body(): everyone = lax.all_gather(residue_feats, 'gx', axis=0, tiled=True)  23.8 us
    all_to_all x1, blocking collectives, body(): lax.all_to_all(whole_rows, 'gx', split_axis=2, concat_axis=1, tiled=True)  16.9 us
    dot_general x18, matrix products, dilated(): jnp.einsum('oc,crw->orw', weights[filter_tap_index], window, preferred_el...  6.34 us
    ppermute x4, starting transfers between devices, with_halo(): lax.ppermute(tail, axis, [(i, (i + 1) % count) for i in range(ends)])  4.94 us
    ppermute x4, starting transfers between devices, with_halo(): lax.ppermute(head, axis, [((i + 1) % count, i) for i in range(ends)])  3.96 us
    ppermute x4, waiting for transfers between devices, with_halo(): lax.ppermute(head, axis, [((i + 1) % count, i) for i in range(ends)])  3.65 us
    concatenate x4, other arithmetic, with_halo(): jnp.concatenate([lax.ppermute(tail, axis, [(i, (i + 1) % count) for i in...  2.87 us
  transfers between devices with their start and end apart: 8, of which 2 were waited for; matrix products, arithmetic and copies ran while one was open for 1% of the time, Pallas kernels for 0%

commit v1 on v0

--- a/solution.py
+++ b/solution.py
@@ -1,6 +1,10 @@
+import functools
+
 import jax
 import jax.numpy as jnp
 from jax import lax
+from jax.experimental import pallas as pl
+from jax.experimental.pallas import tpu as pltpu
 from jax.sharding import PartitionSpec as P
 
 DILATION_STEP = 8
@@ -91,8 +95,362 @@
     )
 
 
+MESH = pl.DeviceIdType.MESH
+D = DILATION_STEP
+BF = jnp.bfloat16
+F32 = jnp.float32
+
+
+def low_half():
+    return lax.broadcasted_iota(jnp.int32, (1, 128), 1) < 64
+
+
+def half_roll(v):
+    return pltpu.roll(v, 64, 1)
+
+
+def three_shifts(v):
+    gap = jnp.zeros((D, v.shape[1]), v.dtype)
+    left = jnp.concatenate([gap, v[:-D]], axis=0)
+    right = jnp.concatenate([v[D:], gap], axis=0)
+    return jnp.concatenate([left.astype(BF), v.astype(BF), right.astype(BF)], axis=1)
+
+
+def times(a, w):
+    return lax.dot_general(a, w, (((1,), (1,)), ((), ())), preferred_element_type=F32)
+
+
+def fold_rows(v):
+    return jnp.sum(v.reshape(v.shape[0] // 8, 8, v.shape[1]), axis=0)
+
+
+def elu(v):
+    return jnp.where(v > 0, v, jnp.exp(jnp.minimum(v, 0.0)) - 1.0)
+
+
+def fused(
+    n,
+    pair_hbm, feats, w_row, w_col, taps1, taps2, scale, shift,
+    out,
+    pair_v, p32, halo_up, halo_dn, h32, all_feats, own_w, halo_w,
+    shifts, acc, send_up, send_dn, got_up, got_dn, stats, block, mirror, m32,
+    in_sem, feat_s, feat_r, halo_s, halo_r, stat_s, stat_r, edge_s, edge_r, mir_s, mir_r,
+):
+    me = lax.axis_index("gx")
+    cols = pair_v.shape[2]
+    cells = float(n * 2 * D * cols)
+    rows = 2 * D
+    ch = pair_v.shape[0]
+    low = low_half()
+
+    barrier = pltpu.get_barrier_semaphore()
+
+    @pl.loop(1, n)
+    def _(k):
+        pl.semaphore_signal(
+            barrier, inc=1, device_id={"gx": lax.rem(me + k, n)}, device_id_type=MESH
+        )
+
+    load = pltpu.make_async_copy(pair_hbm, pair_v, in_sem)
+    load.start()
+
+    for index, taps in enumerate((taps1, taps2)):
+        t = taps[...].astype(F32)
+        none = jnp.zeros_like(t[0])
+        for kx in range(3):
+            where = slice(kx * 128, kx * 128 + 128)
+            top = jnp.concatenate([t[3 + kx], t[6 + kx]], axis=1)
+            bottom = jnp.concatenate([t[kx], t[3 + kx]], axis=1)
+            own_w[index, :, where] = jnp.concatenate([top, bottom], axis=0).astype(BF)
+            top = jnp.concatenate([t[kx], none], axis=1)
+            bottom = jnp.concatenate([none, t[6 + kx]], axis=1)
+            halo_w[index, :, where] = jnp.concatenate([top, bottom], axis=0).astype(BF)
+
+    pl.semaphore_wait(barrier, n - 1)
+
+    def copy_to(src, dst, s, r, peer):
+        return pltpu.make_async_remote_copy(
+            src_ref=src, dst_ref=dst, send_sem=s, recv_sem=r,
+            device_id={"gx": peer}, device_id_type=MESH,
+        )
+
+    above = jnp.maximum(me - 1, 0)
+    below = jnp.minimum(me + 1, n - 1)
+    up1 = copy_to(pair_hbm.at[:, pl.ds(0, D), :], halo_dn, halo_s.at[0], halo_r.at[0], above)
+    dn1 = copy_to(pair_hbm.at[:, pl.ds(D, D), :], halo_up, halo_s.at[1], halo_r.at[1], below)
+
+    def feat_copy(k):
+        return copy_to(
+            feats, all_feats.at[me], feat_s.at[k], feat_r.at[k], lax.rem(me + k, n)
+        )
+
+    def stat_copy(index, k):
+        return copy_to(
+            stats.at[index, me], stats.at[index, me], stat_s.at[index, k], stat_r.at[index, k],
+            lax.rem(me + k, n),
+        )
+
+    def mirror_copy(k):
+        peer = lax.rem(me + k, n)
+        start = pl.multiple_of(peer * rows, rows)
+        return copy_to(
+            block.at[:, pl.ds(start, rows), :], mirror.at[me], mir_s.at[k], mir_r.at[k], peer
+        )
+
+    def edges_start(first, second):
+        @pl.when(me > 0)
+        def _():
+            first.start()
+
+        @pl.when(me < n - 1)
+        def _():
+            second.start()
+
+    def edges_wait_recv(first, second):
+        @pl.when(me < n - 1)
+        def _():
+            first.wait_recv()
+
+        @pl.when(me > 0)
+        def _():
+            second.wait_recv()
+
+    def edges_wait_send(first, second):
+        @pl.when(me > 0)
+        def _():
+            first.wait_send()
+
+        @pl.when(me < n - 1)
+        def _():
+            second.wait_send()
+
+    @pl.loop(1, n)
+    def _(k):
+        feat_copy(k).start()
+
+    edges_start(up1, dn1)
+
+    all_feats[me] = feats[...]
+    load.wait()
+    for h in range(cols // 128):
+        part = pair_v[:, :, h * 128 : h * 128 + 128].astype(F32)
+        p32[h] = part.reshape(ch * rows, 128)
+
+    w_row2 = jnp.concatenate([w_row[...].astype(F32)] * 2, axis=1).astype(BF)
+    w_col2 = jnp.concatenate([w_col[...].astype(F32)] * 2, axis=1).astype(BF)
+
+    def rounded(a, w):
+        return jnp.dot(a, w, preferred_element_type=F32).astype(BF).astype(F32)
+
+    own_rows = rounded(feats[...], w_row2)
+    own_rows = jnp.where(low, own_rows[:D], own_rows[D:])
+
+    @pl.loop(1, n)
+    def _(k):
+        feat_copy(k).wait_recv()
+
+    col_part = rounded(all_feats[...].reshape(n * rows, feats.shape[1]), w_col2)
+    rows_up = rounded(all_feats[above], w_row2)[D:]
+    rows_dn = rounded(all_feats[below], w_row2)[:D]
+    halo_rows = jnp.where(low, rows_up, rows_dn)
+    inside = jnp.where(low, (me > 0).astype(F32), (me < n - 1).astype(F32)) > 0.5
+
+    def pick(values, i):
+        chosen = lax.broadcasted_iota(jnp.int32, values.shape, 0) == i
+        return jnp.sum(jnp.where(chosen, values, 0.0), axis=0, keepdims=True)
+
+    @pl.loop(0, D)
+    def _(i):
+        halves = []
+        for h in range(cols // 128):
+            first = p32[h, pl.ds(i, ch, stride=rows), :]
+            second = p32[h, pl.ds(i + D, ch, stride=rows), :]
+            halves.append(jnp.concatenate([first, second], axis=0).T)
+        v = jnp.concatenate(halves, axis=0) + pick(own_rows, i) + col_part
+        v = v.astype(BF).astype(F32)
+        moved = three_shifts(v)
+        block[i] = v.astype(BF)
+        acc[i] = times(moved, own_w[0])
+
+    edges_wait_recv(up1, dn1)
+    for h in range(cols // 128):
+        where = slice(h * 128, h * 128 + 128)
+        h32[0, h] = halo_up[:, :, where].astype(F32).reshape(ch * D, 128)
+        h32[1, h] = halo_dn[:, :, where].astype(F32).reshape(ch * D, 128)
+
+    zeros = jnp.zeros((8, 128), F32)
+
+    def first_edge(i, sums):
+        halves = []
+        for h in range(cols // 128):
+            first = h32[0, h, pl.ds(i, ch, stride=D), :]
+            second = h32[1, h, pl.ds(i, ch, stride=D), :]
+            halves.append(jnp.concatenate([first, second], axis=0).T)
+        v = jnp.concatenate(halves, axis=0) + pick(halo_rows, i) + col_part
+        v = jnp.where(inside, v, 0.0)
+        a = acc[i] + times(three_shifts(v), halo_w[0])
+        acc[i] = a
+        return sums[0] + fold_rows(a), sums[1] + fold_rows(a * a)
+
+    def publish(index, sums):
+        lines = []
+        for v in sums:
+            v = jnp.sum(v, axis=0, keepdims=True)
+            lines.append(v + half_roll(v))
+        stats[index, me] = jnp.concatenate(lines + [jnp.zeros((6, 128), F32)], axis=0)
+
+        @pl.loop(1, n)
+        def _(k):
+            stat_copy(index, k).start()
+
+    def collect(index):
+        @pl.loop(1, n)
+        def _(k):
+            stat_copy(index, k).wait_recv()
+
+        total = jnp.sum(stats[index], axis=0)
+        average = total[0:1] / cells
+        spread = total[1:2] / cells - average * average
+        gain = jnp.concatenate([scale[index : index + 1, :]] * 2, axis=1)
+        base = jnp.concatenate([shift[index : index + 1, :]] * 2, axis=1)
+        return average, gain * lax.rsqrt(spread + epsilon), base
+
+    sums = lax.fori_loop(0, D, first_edge, (zeros, zeros))
+    publish(0, sums)
+
+    @pl.loop(0, D // 2)
+    def _(i):
+        early, late = acc[i], acc[i + D // 2]
+        send_up[i] = jnp.where(low, early, half_roll(late)).astype(BF)
+        send_dn[i] = jnp.where(low, half_roll(early), late).astype(BF)
+
+    up2 = copy_to(send_up, got_dn, edge_s.at[0], edge_r.at[0], above)
+    dn2 = copy_to(send_dn, got_up, edge_s.at[1], edge_r.at[1], below)
+    edges_start(up2, dn2)
+
+    average, factor, base = collect(0)
+
+    @pl.loop(0, D)
+    def _(i):
+        a = elu((acc[i] - average) * factor + base)
+        acc[i] = times(three_shifts(a), own_w[1])
+
+    edges_wait_recv(up2, dn2)
+
+    def second_edge(i, sums):
+        u = got_up[i].astype(F32)
+        d = got_dn[i].astype(F32)
+        early = jnp.where(low, u, half_roll(d))
+        late = jnp.where(low, half_roll(u), d)
+        for offset, v in ((0, early), (D // 2, late)):
+            v = jnp.where(inside, elu((v - average) * factor + base), 0.0)
+            a = acc[i + offset] + times(three_shifts(v), halo_w[1])
+            acc[i + offset] = a
+            sums = sums[0] + fold_rows(a), sums[1] + fold_rows(a * a)
+        return sums
+
+    sums = lax.fori_loop(0, D // 2, second_edge, (zeros, zeros))
+    publish(1, sums)
+    average, factor, base = collect(1)
+
+    @pl.loop(0, D)
+    def _(i):
+        v = block[i].astype(F32) + (acc[i] - average) * factor + base
+        block[i] = elu(v).astype(BF)
+
+    @pl.loop(1, n)
+    def _(k):
+        mirror_copy(k).start()
+
+    mirror[me] = block[:, pl.ds(pl.multiple_of(me * rows, rows), rows), :]
+
+    @pl.loop(1, n)
+    def _(k):
+        mirror_copy(k).wait_recv()
+
+    @pl.loop(0, n)
+    def _(e):
+        start = pl.multiple_of(e * (D * rows), D * rows)
+        m32[pl.ds(start, D * rows), :] = mirror[e].astype(F32).reshape(D * rows, 128)
+
+    @pl.loop(0, D)
+    def _(i):
+        first = m32[pl.ds(i, n * D, stride=rows), :]
+        second = m32[pl.ds(i + D, n * D, stride=rows), :]
+        even = jnp.where(low, first, half_roll(second)).reshape(n, 1, D, 128)
+        odd = jnp.where(low, half_roll(first), second).reshape(n, 1, D, 128)
+        m = jnp.concatenate([even, odd], axis=1).reshape(cols, 128)
+        v = 0.5 * (block[i].astype(F32) + m)
+        for h in range(cols // 128):
+            t = v[h * 128 : h * 128 + 128].T
+            p32[h, pl.ds(i, ch, stride=rows), :] = t[:ch]
+            p32[h, pl.ds(i + D, ch, stride=rows), :] = t[ch:]
+
+    for h in range(cols // 128):
+        out[:, :, h * 128 : h * 128 + 128] = p32[h].reshape(ch, rows, 128).astype(BF)
+
+    @pl.loop(1, n)
+    def _(k):
+        feat_copy(k).wait_send()
+        stat_copy(0, k).wait_send()
+        stat_copy(1, k).wait_send()
+        mirror_copy(k).wait_send()
+
+    edges_wait_send(up1, dn1)
+    edges_wait_send(up2, dn2)
+
+
+def fused_body(n, *args):
+    residue_feats, pair_feats = args[:2]
+    ch, rows, cols = pair_feats.shape
+    halves = cols // 128
+    vmem = pl.BlockSpec(memory_space=pltpu.VMEM)
+    dma = pltpu.SemaphoreType.DMA
+    return pl.pallas_call(
+        functools.partial(fused, n),
+        out_shape=jax.ShapeDtypeStruct(pair_feats.shape, BF),
+        in_specs=[pl.BlockSpec(memory_space=pl.ANY)] + [vmem] * 7,
+        out_specs=vmem,
+        scratch_shapes=[
+            pltpu.VMEM((ch, rows, cols), BF),
+            pltpu.VMEM((halves, ch * rows, 128), F32),
+            pltpu.VMEM((ch, D, cols), BF),
+            pltpu.VMEM((ch, D, cols), BF),
+            pltpu.VMEM((2, halves, ch * D, 128), F32),
+            pltpu.VMEM((n,) + residue_feats.shape, BF),
+            pltpu.VMEM((2, 128, 384), BF),
+            pltpu.VMEM((2, 128, 384), BF),
+            pltpu.VMEM((8, 128), F32),
+            pltpu.VMEM((D, cols, 128), F32),
+            pltpu.VMEM((D // 2, cols, 128), BF),
+            pltpu.VMEM((D // 2, cols, 128), BF),
+            pltpu.VMEM((D // 2, cols, 128), BF),
+            pltpu.VMEM((D // 2, cols, 128), BF),
+            pltpu.VMEM((2, n, 8, 128), F32),
+            pltpu.VMEM((D, cols, 128), BF),
+            pltpu.VMEM((n, D, rows, 128), BF),
+            pltpu.VMEM((n * D * rows, 128), F32),
+            dma,
+            dma((n,)), dma((n,)), dma((2,)), dma((2,)), dma((2, n)), dma((2, n)),
+            dma((2,)), dma((2,)), dma((n,)), dma((n,)),
+        ],
+        compiler_params=pltpu.CompilerParams(
+            collective_id=0, has_side_effects=True, vmem_limit_bytes=40 * 1024 * 1024
+        ),
+    )(pair_feats, residue_feats, *args[2:])
+
+
 def solution(mesh):
     placed = (P(("grp", "gx"), None), P(None, ("grp", "gx"), "gy"), P(), P(), P(), P(), P(), P())
+    n = mesh.shape["gx"]
+
+    def chosen(*args):
+        ch, rows, cols = args[1].shape
+        fits = mesh.shape["gy"] == 1 and rows == 2 * D and cols == n * rows
+        if fits and ch == 64 and cols % 128 == 0 and cols <= 512:
+            return fused_body(n, *args)
+        return body(*args)
+
     return jax.shard_map(
-        body, mesh=mesh, in_specs=placed, out_specs=P(None, ("grp", "gx"), "gy"), check_vma=False
-    )
+        chosen, mesh=mesh, in_specs=placed, out_specs=P(None, ("grp", "gx"), "gy"), check_vma=False
+    )

time: 141 us -> 49.4 us (0.35)
  the two profiles are of different devices: /device:TPU:0 before, /device:TPU:15 now
where the time goes in v1:
time: 49.4 us; the launch traced here: 49.2 us
  Pallas kernels  44.5 us (90%)
  local copies, waits for them, and re-layouts  4.56 us (9%)
    pallas_call x1, Pallas kernels, fused_body(): pl.pallas_call(functools.partial(fused, n), out_shape=jax.ShapeDtypeStruc...  44.5 us
    unnamed x15, local copies, waits for them, and re-layouts  4.56 us

profile of v1, /device:TPU:15, one launch (start us, length us, event | category | flops | bytes accessed | tf_op | source)
XLA Modules:
  0.0 49.2 jit_solution(7908421140592726317)
XLA Ops:
  0.0 0.0 copy-start.1
  0.0 0.9 %copy.9.w_row = bf16[256,64]{1,0:T(8,128)(2,1)S(1)} copy(bf16[256,64]{0,1:T(8,128)(2,1)} %param.10) | data formatting | bytes 65536 | tf_op args[2]
  0.9 0.0 copy-start.3
  0.9 0.0 copy-start.4
  0.9 0.0 copy-start.5
  0.9 0.9 %copy.10.w_col = bf16[256,64]{1,0:T(8,128)(2,1)S(1)} copy(bf16[256,64]{0,1:T(8,128)(2,1)} %param.11) | data formatting | bytes 65536 | tf_op args[3]
  1.8 0.0 copy-done.1
  1.8 0.0 copy-done.3
  1.9 0.0 copy-done.4
  1.9 0.0 copy-done.5
  1.9 0.0 copy-start
  1.9 1.0 %copy-done = bf16[64,16,256]{2,1,0:T(8,128)(2,1)S(1)} copy-done((bf16[64,16,256]{2,1,0:T(8,128)(2,1)S(1)}, bf16[64,16,256]{2,1,0:T(8,128)(2,1)}, u32[]{:S(2)}) %copy-start) | copy-done | bytes 524312
  2.9 0.0 copy-start.2
  2.9 0.9 %copy-done.2 = bf16[9,64,64]{2,1,0:T(8,128)(2,1)S(1)} copy-done((bf16[9,64,64]{2,1,0:T(8,128)(2,1)S(1)}, bf16[9,64,64]{2,1,0:T(8,128)(2,1)}, u32[]{:S(2)}) %copy-start.2) | copy-done | bytes 73752
  3.8 44.5 %shard_map.82 = bf16[64,16,256]{2,1,0:T(8,128)(2,1)S(1)} custom-call(bf16[64,16,256]{2,1,0:T(8,128)(2,1)S(1)} %copy-done, bf16[16,256]{1,0:T(8,128)(2,1)S(1)} %copy-done.3, bf16[256,64]{1,0:T(8,128)(2,1)S(1)} %copy.9.w_row, bf16[256,64]{1,0:T(8,128)(2,1)S(1)} %copy.10.w_col, bf16[9,64,64]{2,1,0:T(8,128)(2,1)S(1)} %copy-done.1, ...), custom_call_target="tpu_custom_call" | custom-call | tf_op jit(solution)/shard_map/pallas_call | solution.py:409
  48.4 0.8 %copy.12 = bf16[64,16,256]{2,1,0:T(8,128)(2,1)} copy(bf16[64,16,256]{2,1,0:T(8,128)(2,1)S(1)} %shard_map.82) | data formatting | bytes 1048576
Async XLA Ops:
  0.0 1.8 %copy-start.1 = (bf16[9,64,64]{2,1,0:T(8,128)(2,1)S(1)}, bf16[9,64,64]{2,1,0:T(8,128)(2,1)}, u32[]{:S(2)}) copy-start(bf16[9,64,64]{2,1,0:T(8,128)(2,1)} %taps1.1) | copy-start | bytes 221188
  0.9 0.9 %copy-start.3 = (bf16[16,256]{1,0:T(8,128)(2,1)S(1)}, bf16[16,256]{1,0:T(8,128)(2,1)}, u32[]{:S(2)}) copy-start(bf16[16,256]{1,0:T(8,128)(2,1)} %feats.1) | copy-start | bytes 24580
  0.9 0.9 %copy-start.4 = (f32[2,64]{1,0:T(2,128)S(1)}, f32[2,64]{1,0:T(2,128)}, u32[]{:S(2)}) copy-start(f32[2,64]{1,0:T(2,128)} %scale.1) | copy-start | bytes 1540
  0.9 0.9 %copy-start.5 = (f32[2,64]{1,0:T(2,128)S(1)}, f32[2,64]{1,0:T(2,128)}, u32[]{:S(2)}) copy-start(f32[2,64]{1,0:T(2,128)} %shift.1) | copy-start | bytes 1540
  1.9 1.0 %copy-start = (bf16[64,16,256]{2,1,0:T(8,128)(2,1)S(1)}, bf16[64,16,256]{2,1,0:T(8,128)(2,1)}, u32[]{:S(2)}) copy-start(bf16[64,16,256]{2,1,0:T(8,128)(2,1)} %pair_hbm.1) | copy-start | bytes 1572868
  2.9 0.9 %copy-start.2 = (bf16[9,64,64]{2,1,0:T(8,128)(2,1)S(1)}, bf16[9,64,64]{2,1,0:T(8,128)(2,1)}, u32[]{:S(2)}) copy-start(bf16[9,64,64]{2,1,0:T(8,128)(2,1)} %taps2.1) | copy-start | bytes 221188

commit v2 on v1

v2 whole, which is shorter than its diff:
```python
import functools

import jax
import jax.numpy as jnp
from jax import lax
from jax.experimental import pallas as pl
from jax.experimental.pallas import tpu as pltpu
from jax.sharding import PartitionSpec as P

DILATION_STEP = 8


epsilon = 1e-05


def with_halo(cells, sides, width):
    for axis, dim in sides:
        count = lax.axis_size(axis)
        ends = count - 1
        head = lax.slice_in_dim(cells, 0, width, axis=dim)
        tail = lax.slice_in_dim(cells, cells.shape[dim] - width, cells.shape[dim], axis=dim)
        cells = jnp.concatenate(
            [
                lax.ppermute(tail, axis, [(i, (i + 1) % count) for i in range(ends)]),
                cells,
                lax.ppermute(head, axis, [((i + 1) % count, i) for i in range(ends)]),
            ],
            axis=dim,
        )
    return cells


def dilated(receptive_region, weights):
    row_count = receptive_region.shape[1]
    col_count = receptive_region.shape[2]
    border_padded_input = with_halo(receptive_region, (("gx", 1), ("gy", 2)), DILATION_STEP)
    tap_sum_total = jnp.zeros((weights.shape[1], row_count, col_count), jnp.float32)
    for filter_tap_index in range(9):
        row_displacement = filter_tap_index // 3 * DILATION_STEP
        column_displacement = filter_tap_index % 3 * DILATION_STEP
        window = border_padded_input[
            :,
            row_displacement : row_displacement + row_count,
            column_displacement : column_displacement + col_count,
        ]
        tap_sum_total = tap_sum_total + jnp.einsum(
            "oc,crw->orw", weights[filter_tap_index], window, preferred_element_type=jnp.float32
        )
    return tap_sum_total


def normalized(tap_sum_total, gain, shift):
    cell_count = (
        tap_sum_total.shape[1] * tap_sum_total.shape[2] * lax.axis_size("gx") * lax.axis_size("gy")
    )
    first_sum, second_sum = lax.psum(
        (jnp.sum(tap_sum_total, axis=(1, 2)), jnp.sum(tap_sum_total * tap_sum_total, axis=(1, 2))),
        ("gx", "gy"),
    )
    average = first_sum / cell_count
    spread = second_sum / cell_count - average * average
    centred = tap_sum_total - average[:, None, None]
    factor = gain * lax.rsqrt(spread + epsilon)
    return centred * factor[:, None, None] + shift[:, None, None]


def body(residue_feats, pair_feats, w_row, w_col, first_taps, second_taps, norm_scale, norm_shift):
    col_count = pair_feats.shape[2]
    col_start = lax.axis_index("gy") * col_count
    row_part = jnp.dot(residue_feats, w_row, preferred_element_type=jnp.float32).astype(
        jnp.bfloat16
    )
    everyone = lax.all_gather(residue_feats, "gx", axis=0, tiled=True)
    col_feats = lax.dynamic_slice_in_dim(everyone, col_start, col_count, 0)
    col_part = jnp.dot(col_feats, w_col, preferred_element_type=jnp.float32).astype(jnp.bfloat16)
    block_in = (
        pair_feats.astype(jnp.float32)
        + row_part.T.astype(jnp.float32)[:, :, None]
        + col_part.T.astype(jnp.float32)[:, None, :]
    ).astype(jnp.bfloat16)
    first_conv = dilated(block_in, first_taps)
    activated = jax.nn.elu(normalized(first_conv, norm_scale[0], norm_shift[0])).astype(
        jnp.bfloat16
    )
    second_conv = dilated(activated, second_taps)
    block_out = jax.nn.elu(
        block_in.astype(jnp.float32) + normalized(second_conv, norm_scale[1], norm_shift[1])
    ).astype(jnp.bfloat16)
    whole_rows = lax.all_gather(block_out, "gy", axis=2, tiled=True)
    columns = lax.all_to_all(whole_rows, "gx", split_axis=2, concat_axis=1, tiled=True)
    flipped = lax.dynamic_slice_in_dim(columns, col_start, col_count, 1)
    mirrored = jnp.transpose(flipped, (0, 2, 1))
    return (0.5 * (block_out.astype(jnp.float32) + mirrored.astype(jnp.float32))).astype(
        jnp.bfloat16
    )


MESH = pl.DeviceIdType.MESH
D = DILATION_STEP
BF = jnp.bfloat16
F32 = jnp.float32


def low_half():
    return lax.broadcasted_iota(jnp.int32, (1, 128), 1) < 64


def half_roll(v):
    return pltpu.roll(v, 64, 1)


def three_shifts(v):
    gap = jnp.zeros((D, v.shape[1]), v.dtype)
    left = jnp.concatenate([gap, v[:-D]], axis=0)
    right = jnp.concatenate([v[D:], gap], axis=0)
    return jnp.concatenate([left.astype(BF), v.astype(BF), right.astype(BF)], axis=1)


def times(a, w):
    return lax.dot_general(a, w, (((1,), (1,)), ((), ())), preferred_element_type=F32)


def fold_rows(v):
    return jnp.sum(v.reshape(v.shape[0] // 8, 8, v.shape[1]), axis=0)


def elu(v):
    return jnp.where(v > 0, v, jnp.exp(jnp.minimum(v, 0.0)) - 1.0)


def fused(
    n,
    pair_hbm, feats_hbm, w_row_hbm, w_col_hbm, taps1_hbm, taps2_hbm, scale_hbm, shift_hbm,
    out,
    feats, w_row, w_col, taps1, taps2, scale, shift,
    pair, p32, all_feats, own_w, halo_w, col_conv, col_base, acc,
    edges, stats, block, mirror, m32, out_v,
    in_sem, feat_s, feat_r, stat_s, stat_r, edge_s, edge_r, mir_s, mir_r, out_sem,
):
    me = lax.axis_index("gx")
    ch, rows, cols = pair.shape
    half = n // 2
    side = lax.div(me, half)
    lane = lax.rem(me, half)
    cells = float(n * rows * cols)
    low = low_half()

    def peer_of(k):
        return lax.rem(side + 1 + lax.div(k, half), 2) * half + lax.rem(lane + k, half)

    def sender_of(k):
        return lax.rem(side + 1 + lax.div(k, half), 2) * half + lax.rem(lane + n - k, half)

    def far_peers(act):
        pl.loop(0, half)(act)

    def near_peers(act):
        pl.loop(half + 1, n)(act)

    def all_peers(act):
        far_peers(act)
        near_peers(act)

    barrier = pltpu.get_barrier_semaphore()

    @all_peers
    def _(k):
        pl.semaphore_signal(barrier, inc=1, device_id={"gx": peer_of(k)}, device_id_type=MESH)

    loads = [
        pltpu.make_async_copy(src, dst, in_sem.at[k])
        for k, (src, dst) in enumerate(
            (
                (feats_hbm, feats), (w_row_hbm, w_row), (pair_hbm, pair), (w_col_hbm, w_col),
                (taps1_hbm, taps1), (taps2_hbm, taps2), (scale_hbm, scale), (shift_hbm, shift),
            )
        )
    ]
    for load in loads:
        load.start()
    for load in loads:
        load.wait()

    def rounded(a, w):
        return times(a, w).astype(BF).astype(F32)

    w_row2 = jnp.concatenate([w_row[...]] * 2, axis=0)
    w_col2 = jnp.concatenate([w_col[...]] * 2, axis=0)
    own_rows = rounded(feats[...], w_row2)
    own_rows = jnp.where(low, own_rows[:D], own_rows[D:])
    halves = cols // 128
    for h in range(halves):
        part = pair[:, :, h * 128 : h * 128 + 128].astype(F32)
        p32[h] = part.reshape(ch * rows, 128)

    def pick(values, i):
        chosen = lax.broadcasted_iota(jnp.int32, values.shape, 0) == i
        return jnp.sum(jnp.where(chosen, values, 0.0), axis=0, keepdims=True)

    def with_rows(i):
        parts = []
        for h in range(halves):
            first = p32[h, pl.ds(i, ch, stride=rows), :]
            second = p32[h, pl.ds(i + D, ch, stride=rows), :]
            parts.append(jnp.concatenate([first, second], axis=0).T)
        return jnp.concatenate(parts, axis=0) + pick(own_rows, i)

    def pack(index, i, early, late):
        edges[index, 0, i] = jnp.where(low, early, half_roll(late)).astype(BF)
        edges[index, 1, i] = jnp.where(low, half_roll(early), late).astype(BF)

    @pl.loop(0, D // 2)
    def _(i):
        early, late = with_rows(i), with_rows(i + D // 2)
        block[i] = early.astype(BF)
        block[i + D // 2] = late.astype(BF)
        pack(0, i, early, late)

    for index, taps in enumerate((taps1, taps2)):
        t = taps[...].astype(F32)
        none = jnp.zeros_like(t[0])
        for kx in range(3):
            where = slice(kx * 128, kx * 128 + 128)
            top = jnp.concatenate([t[3 + kx], t[6 + kx]], axis=1)
            bottom = jnp.concatenate([t[kx], t[3 + kx]], axis=1)
            own_w[index, :, where] = jnp.concatenate([top, bottom], axis=0).astype(BF)
            top = jnp.concatenate([t[kx], none], axis=1)
            bottom = jnp.concatenate([none, t[6 + kx]], axis=1)
            halo_w[index, :, where] = jnp.concatenate([top, bottom], axis=0).astype(BF)

    pl.semaphore_wait(barrier, n - 1)

    def copy_to(src, dst, s, r, peer):
        return pltpu.make_async_remote_copy(
            src_ref=src, dst_ref=dst, send_sem=s, recv_sem=r,
            device_id={"gx": peer}, device_id_type=MESH,
        )

    def feat_copy(k):
        return copy_to(feats, all_feats.at[me], feat_s.at[k], feat_r.at[k], peer_of(k))

    def stat_copy(index, k):
        return copy_to(
            stats.at[index, me], stats.at[index, me], stat_s.at[index, k], stat_r.at[index, k],
            peer_of(k),
        )

    def mirror_copy(k):
        peer = peer_of(k)
        start = pl.multiple_of(peer * rows, rows)
        return copy_to(
            block.at[:, pl.ds(start, rows), :], mirror.at[me], mir_s.at[k], mir_r.at[k], peer
        )

    def edge_copies(index):
        above, below = jnp.maximum(me - 1, 0), jnp.minimum(me + 1, n - 1)
        s, r = edge_s.at[index], edge_r.at[index]
        return (
            copy_to(edges.at[index, 0], edges.at[index, 3], s.at[0], r.at[0], above),
            copy_to(edges.at[index, 1], edges.at[index, 2], s.at[1], r.at[1], below),
        )

    def edges_start(index):
        first, second = edge_copies(index)

        @pl.when(me > 0)
        def _():
            first.start()

        @pl.when(me < n - 1)
        def _():
            second.start()

    def edges_wait_recv(index):
        first, second = edge_copies(index)

        @pl.when(me < n - 1)
        def _():
            first.wait_recv()

        @pl.when(me > 0)
        def _():
            second.wait_recv()

    def edges_wait_send(index):
        first, second = edge_copies(index)

        @pl.when(me > 0)
        def _():
            first.wait_send()

        @pl.when(me < n - 1)
        def _():
            second.wait_send()

    @all_peers
    def _(k):
        feat_copy(k).start()

    edges_start(0)
    all_feats[me] = feats[...]

    @pl.loop(0, D)
    def _(i):
        acc[i] = times(three_shifts(block[i].astype(F32)), own_w[0])

    @all_peers
    def _(k):
        feat_copy(k).wait_recv()

    inside = jnp.where(low, (me > 0).astype(F32), (me < n - 1).astype(F32)) > 0.5
    col_part = rounded(all_feats[...].reshape(n * rows, feats.shape[1]), w_col2)
    col_conv[...] = times(three_shifts(col_part), own_w[0]) + times(
        three_shifts(jnp.where(inside, col_part, 0.0)), halo_w[0]
    )
    col_base[...] = col_part + jnp.concatenate([shift[1:2, :]] * 2, axis=1)

    def unpacked(index, i):
        u = edges[index, 2, i].astype(F32)
        d = edges[index, 3, i].astype(F32)
        return jnp.where(low, u, half_roll(d)), jnp.where(low, half_roll(u), d)

    def add_sums(sums, a):
        return sums[0] + fold_rows(a), sums[1] + fold_rows(a * a)

    zeros = jnp.zeros((8, 128), F32)

    def publish(index, sums):
        lines = []
        for v in sums:
            v = jnp.sum(v, axis=0, keepdims=True)
            lines.append(v + half_roll(v))
        stats[index, me] = jnp.concatenate(lines + [jnp.zeros((6, 128), F32)], axis=0)

        @all_peers
        def _(k):
            stat_copy(index, k).start()

    def collect(index):
        @all_peers
        def _(k):
            stat_copy(index, k).wait_recv()

        total = jnp.sum(stats[index], axis=0)
        average = total[0:1] / cells
        spread = total[1:2] / cells - average * average
        gain = jnp.concatenate([scale[index : index + 1, :]] * 2, axis=1)
        return average, gain * lax.rsqrt(spread + epsilon)

    edges_wait_recv(0)

    def first_edge(i, sums):
        results = []
        for offset, v in zip((0, D // 2), unpacked(0, i)):
            v = jnp.where(inside, v, 0.0)
            a = acc[i + offset] + times(three_shifts(v), halo_w[0]) + col_conv[...]
            acc[i + offset] = a
            sums = add_sums(sums, a)
            results.append(a)
        pack(1, i, *results)
        return sums

    sums = lax.fori_loop(0, D // 2, first_edge, (zeros, zeros))
    publish(0, sums)
    edges_start(1)
    average, factor = collect(0)
    base = jnp.concatenate([shift[0:1, :]] * 2, axis=1)

    @pl.loop(0, D)
    def _(i):
        a = elu((acc[i] - average) * factor + base)
        acc[i] = times(three_shifts(a), own_w[1])

    edges_wait_recv(1)

    def second_edge(i, sums):
        for offset, v in zip((0, D // 2), unpacked(1, i)):
            v = jnp.where(inside, elu((v - average) * factor + base), 0.0)
            a = acc[i + offset] + times(three_shifts(v), halo_w[1])
            acc[i + offset] = a
            sums = add_sums(sums, a)
        return sums

    sums = lax.fori_loop(0, D // 2, second_edge, (zeros, zeros))
    publish(1, sums)
    average2, factor2 = collect(1)

    def result_of(which):
        where = pl.ds(pl.multiple_of(which * 128, 128), 128)

        @pl.loop(0, D)
        def _(i):
            v = block[i, where, :].astype(F32) + col_base[where, :]
            v = v + (acc[i, where, :] - average2) * factor2
            block[i, where, :] = elu(v).astype(BF)

    def widen(e):
        start = pl.multiple_of(e * (D * rows), D * rows)
        m32[pl.ds(start, D * rows), :] = mirror[e].astype(F32).reshape(D * rows, 128)

    def finish(which):
        where = pl.ds(pl.multiple_of(which * 128, 128), 128)
        offset = which * (half * D * rows)

        @pl.loop(0, D)
        def _(i):
            first = m32[pl.ds(offset + i, half * D, stride=rows), :]
            second = m32[pl.ds(offset + i + D, half * D, stride=rows), :]
            even = jnp.where(low, first, half_roll(second)).reshape(half, 1, D, 128)
            odd = jnp.where(low, half_roll(first), second).reshape(half, 1, D, 128)
            m = jnp.concatenate([even, odd], axis=1).reshape(128, 128)
            t = (0.5 * (block[i, where, :].astype(F32) + m)).T
            p32[which, pl.ds(i, ch, stride=rows), :] = t[:ch]
            p32[which, pl.ds(i + D, ch, stride=rows), :] = t[ch:]

        out_v[which] = p32[which].reshape(ch, rows, 128).astype(BF)
        copy = pltpu.make_async_copy(out_v.at[which], out.at[:, :, where], out_sem.at[which])
        copy.start()
        return copy

    result_of(1 - side)

    @far_peers
    def _(k):
        mirror_copy(k).start()

    result_of(side)

    @near_peers
    def _(k):
        mirror_copy(k).start()

    mirror[me] = block[:, pl.ds(pl.multiple_of(me * rows, rows), rows), :]
    widen(me)

    @near_peers
    def _(k):
        mirror_copy(k).wait_recv()
        widen(sender_of(k))

    near = finish(side)

    @all_peers
    def _(k):
        feat_copy(k).wait_send()
        stat_copy(0, k).wait_send()
        stat_copy(1, k).wait_send()

    edges_wait_send(0)
    edges_wait_send(1)

    @far_peers
    def _(k):
        mirror_copy(k).wait_recv()
        widen(sender_of(k))

    far = finish(1 - side)

    @all_peers
    def _(k):
        mirror_copy(k).wait_send()

    near.wait()
    far.wait()


def fused_body(n, *args):
    residue_feats, pair_feats = args[:2]
    ch, rows, cols = pair_feats.shape
    halves = cols // 128
    rest = (args[2].T, args[3].T) + args[4:]
    dma = pltpu.SemaphoreType.DMA
    return pl.pallas_call(
        functools.partial(fused, n),
        out_shape=jax.ShapeDtypeStruct(pair_feats.shape, BF),
        in_specs=[pl.BlockSpec(memory_space=pltpu.HBM)] * 8,
        out_specs=pl.BlockSpec(memory_space=pl.ANY),
        scratch_shapes=[
            *[pltpu.VMEM(a.shape, a.dtype) for a in (residue_feats,) + rest],
            pltpu.VMEM((ch, rows, cols), BF),
            pltpu.VMEM((halves, ch * rows, 128), F32),
            pltpu.VMEM((n,) + residue_feats.shape, BF),
            pltpu.VMEM((2, 128, 384), BF),
            pltpu.VMEM((2, 128, 384), BF),
            pltpu.VMEM((cols, 128), F32),
            pltpu.VMEM((cols, 128), F32),
            pltpu.VMEM((D, cols, 128), F32),
            pltpu.VMEM((2, 4, D // 2, cols, 128), BF),
            pltpu.VMEM((2, n, 8, 128), F32),
            pltpu.VMEM((D, cols, 128), BF),
            pltpu.VMEM((n, D, rows, 128), BF),
            pltpu.VMEM((n * D * rows, 128), F32),
            pltpu.VMEM((halves, ch, rows, 128), BF),
            dma((8,)),
            dma((n,)), dma((n,)), dma((2, n)), dma((2, n)), dma((2, 2)), dma((2, 2)),
            dma((n,)), dma((n,)), dma((2,)),
        ],
        compiler_params=pltpu.CompilerParams(
            collective_id=0, has_side_effects=True, vmem_limit_bytes=63 * 1024 * 1024
        ),
    )(pair_feats, residue_feats, *rest)


def solution(mesh):
    placed = (P(("grp", "gx"), None), P(None, ("grp", "gx"), "gy"), P(), P(), P(), P(), P(), P())
    n = mesh.shape["gx"]

    def chosen(*args):
        ch, rows, cols = args[1].shape
        fits = mesh.shape["gy"] == 1 and rows == 2 * D and cols == n * rows
        if fits and ch == 64 and cols == 256:
            return fused_body(n, *args)
        return body(*args)

    return jax.shard_map(
        chosen, mesh=mesh, in_specs=placed, out_specs=P(None, ("grp", "gx"), "gy"), check_vma=False
    )
```

time: 49.4 us -> 48.1 us (0.974)
  the two profiles are of different devices: /device:TPU:15 before, /device:TPU:0 now
where the time goes in v2:
time: 48.1 us; the launch traced here: 47.9 us
  Pallas kernels  46 us (96%)
  local copies, waits for them, and re-layouts  1.87 us (4%)
    pallas_call x1, Pallas kernels, fused_body(): pl.pallas_call(functools.partial(fused, n), out_shape=jax.ShapeDtypeStruc...  46 us
    unnamed x1, local copies, waits for them, and re-layouts  1.87 us

profile of v2, /device:TPU:0, one launch (start us, length us, event | category | flops | bytes accessed | tf_op | source)
XLA Modules:
  0.0 47.9 jit_solution(15539180655641998400)
XLA Ops:
  0.0 46.0 %shard_map.82 = bf16[64,16,256]{2,1,0:T(8,128)(2,1)} custom-call(bf16[64,16,256]{2,1,0:T(8,128)(2,1)} %pair_hbm.1, bf16[16,256]{1,0:T(8,128)(2,1)} %feats_hbm.1, bf16[64,256]{1,0:T(8,128)(2,1)} %bitcast.2, bf16[64,256]{1,0:T(8,128)(2,1)} %bitcast.3, bf16[9,64,64]{2,1,0:T(8,128)(2,1)} %taps1_hbm.1, bf16[9,64,64]{2,1,0:T(8,128)(2,1)} %taps2_hbm.1, ...), custom_call_target="tpu_custom_call" | custom-call | tf_op jit(solution)/shard_map/pallas_call | solution.py:473
  46.0 1.9 %copy.10 = bf16[64,16,256]{2,1,0:T(8,128)(2,1)} copy(bf16[64,16,256]{2,1,0:T(8,128)(2,1)} %shard_map.82) | data formatting | bytes 1048576

commit v3 on v2

--- a/solution.py
+++ b/solution.py
@@ -133,12 +133,13 @@
     pair_hbm, feats_hbm, w_row_hbm, w_col_hbm, taps1_hbm, taps2_hbm, scale_hbm, shift_hbm,
     out,
     feats, w_row, w_col, taps1, taps2, scale, shift,
-    pair, p32, all_feats, own_w, halo_w, col_conv, col_base, acc,
-    edges, stats, block, mirror, m32, out_v,
+    pair_up, pair_dn, halo_up, halo_dn, p32, h32, all_feats, own_w, halo_w, col_conv, col_base, acc,
+    edges, stats, block, mirror, m32, o32, out_v,
     in_sem, feat_s, feat_r, stat_s, stat_r, edge_s, edge_r, mir_s, mir_r, out_sem,
 ):
     me = lax.axis_index("gx")
-    ch, rows, cols = pair.shape
+    ch, _, cols = pair_up.shape
+    rows = 2 * D
     half = n // 2
     side = lax.div(me, half)
     lane = lax.rem(me, half)
@@ -171,14 +172,94 @@
         pltpu.make_async_copy(src, dst, in_sem.at[k])
         for k, (src, dst) in enumerate(
             (
-                (feats_hbm, feats), (w_row_hbm, w_row), (pair_hbm, pair), (w_col_hbm, w_col),
+                (feats_hbm, feats), (pair_hbm.at[:, pl.ds(0, D), :], pair_up),
+                (pair_hbm.at[:, pl.ds(D, D), :], pair_dn), (w_row_hbm, w_row), (w_col_hbm, w_col),
                 (taps1_hbm, taps1), (taps2_hbm, taps2), (scale_hbm, scale), (shift_hbm, shift),
             )
         )
     ]
     for load in loads:
         load.start()
-    for load in loads:
+    for load in loads[:3]:
+        load.wait()
+    pl.semaphore_wait(barrier, n - 1)
+
+    def copy_to(src, dst, s, r, peer):
+        return pltpu.make_async_remote_copy(
+            src_ref=src, dst_ref=dst, send_sem=s, recv_sem=r,
+            device_id={"gx": peer}, device_id_type=MESH,
+        )
+
+    def feat_copy(k):
+        return copy_to(feats, all_feats.at[me], feat_s.at[k], feat_r.at[k], peer_of(k))
+
+    def stat_copy(index, k):
+        return copy_to(
+            stats.at[index, me], stats.at[index, me], stat_s.at[index, k], stat_r.at[index, k],
+            peer_of(k),
+        )
+
+    def mirror_copy(k):
+        peer = peer_of(k)
+        start = pl.multiple_of(peer * rows, rows)
+        return copy_to(
+            block.at[:, pl.ds(start, rows), :], mirror.at[me], mir_s.at[k], mir_r.at[k], peer
+        )
+
+    def edge_copies(index):
+        above, below = jnp.maximum(me - 1, 0), jnp.minimum(me + 1, n - 1)
+        s, r = edge_s.at[index], edge_r.at[index]
+        if index == 0:
+            return (
+                copy_to(pair_up, halo_dn, s.at[0], r.at[0], above),
+                copy_to(pair_dn, halo_up, s.at[1], r.at[1], below),
+            )
+        return (
+            copy_to(edges.at[0], edges.at[3], s.at[0], r.at[0], above),
+            copy_to(edges.at[1], edges.at[2], s.at[1], r.at[1], below),
+        )
+
+    def edges_start(index):
+        first, second = edge_copies(index)
+
+        @pl.when(me > 0)
+        def _():
+            first.start()
+
+        @pl.when(me < n - 1)
+        def _():
+            second.start()
+
+    def edges_wait_recv(index):
+        first, second = edge_copies(index)
+
+        @pl.when(me < n - 1)
+        def _():
+            first.wait_recv()
+
+        @pl.when(me > 0)
+        def _():
+            second.wait_recv()
+
+    def edges_wait_send(index):
+        first, second = edge_copies(index)
+
+        @pl.when(me > 0)
+        def _():
+            first.wait_send()
+
+        @pl.when(me < n - 1)
+        def _():
+            second.wait_send()
+
+    @all_peers
+    def _(k):
+        feat_copy(k).start()
+
+    edges_start(0)
+    all_feats[me] = feats[...]
+
+    for load in loads[3:]:
         load.wait()
 
     def rounded(a, w):
@@ -190,31 +271,25 @@
     own_rows = jnp.where(low, own_rows[:D], own_rows[D:])
     halves = cols // 128
     for h in range(halves):
-        part = pair[:, :, h * 128 : h * 128 + 128].astype(F32)
-        p32[h] = part.reshape(ch * rows, 128)
+        where = slice(h * 128, h * 128 + 128)
+        p32[h, 0] = pair_up[:, :, where].astype(F32).reshape(ch * D, 128)
+        p32[h, 1] = pair_dn[:, :, where].astype(F32).reshape(ch * D, 128)
 
     def pick(values, i):
         chosen = lax.broadcasted_iota(jnp.int32, values.shape, 0) == i
         return jnp.sum(jnp.where(chosen, values, 0.0), axis=0, keepdims=True)
 
-    def with_rows(i):
+    def with_rows(source, row_values, i):
         parts = []
         for h in range(halves):
-            first = p32[h, pl.ds(i, ch, stride=rows), :]
-            second = p32[h, pl.ds(i + D, ch, stride=rows), :]
+            first = source[h, 0, pl.ds(i, ch, stride=D), :]
+            second = source[h, 1, pl.ds(i, ch, stride=D), :]
             parts.append(jnp.concatenate([first, second], axis=0).T)
-        return jnp.concatenate(parts, axis=0) + pick(own_rows, i)
-
-    def pack(index, i, early, late):
-        edges[index, 0, i] = jnp.where(low, early, half_roll(late)).astype(BF)
-        edges[index, 1, i] = jnp.where(low, half_roll(early), late).astype(BF)
-
-    @pl.loop(0, D // 2)
-    def _(i):
-        early, late = with_rows(i), with_rows(i + D // 2)
-        block[i] = early.astype(BF)
-        block[i + D // 2] = late.astype(BF)
-        pack(0, i, early, late)
+        return jnp.concatenate(parts, axis=0) + pick(row_values, i)
+
+    def pack(i, early, late):
+        edges[0, i] = jnp.where(low, early, half_roll(late)).astype(BF)
+        edges[1, i] = jnp.where(low, half_roll(early), late).astype(BF)
 
     for index, taps in enumerate((taps1, taps2)):
         t = taps[...].astype(F32)
@@ -228,81 +303,11 @@
             bottom = jnp.concatenate([none, t[6 + kx]], axis=1)
             halo_w[index, :, where] = jnp.concatenate([top, bottom], axis=0).astype(BF)
 
-    pl.semaphore_wait(barrier, n - 1)
-
-    def copy_to(src, dst, s, r, peer):
-        return pltpu.make_async_remote_copy(
-            src_ref=src, dst_ref=dst, send_sem=s, recv_sem=r,
-            device_id={"gx": peer}, device_id_type=MESH,
-        )
-
-    def feat_copy(k):
-        return copy_to(feats, all_feats.at[me], feat_s.at[k], feat_r.at[k], peer_of(k))
-
-    def stat_copy(index, k):
-        return copy_to(
-            stats.at[index, me], stats.at[index, me], stat_s.at[index, k], stat_r.at[index, k],
-            peer_of(k),
-        )
-
-    def mirror_copy(k):
-        peer = peer_of(k)
-        start = pl.multiple_of(peer * rows, rows)
-        return copy_to(
-            block.at[:, pl.ds(start, rows), :], mirror.at[me], mir_s.at[k], mir_r.at[k], peer
-        )
-
-    def edge_copies(index):
-        above, below = jnp.maximum(me - 1, 0), jnp.minimum(me + 1, n - 1)
-        s, r = edge_s.at[index], edge_r.at[index]
-        return (
-            copy_to(edges.at[index, 0], edges.at[index, 3], s.at[0], r.at[0], above),
-            copy_to(edges.at[index, 1], edges.at[index, 2], s.at[1], r.at[1], below),
-        )
-
-    def edges_start(index):
-        first, second = edge_copies(index)
-
-        @pl.when(me > 0)
-        def _():
-            first.start()
-
-        @pl.when(me < n - 1)
-        def _():
-            second.start()
-
-    def edges_wait_recv(index):
-        first, second = edge_copies(index)
-
-        @pl.when(me < n - 1)
-        def _():
-            first.wait_recv()
-
-        @pl.when(me > 0)
-        def _():
-            second.wait_recv()
-
-    def edges_wait_send(index):
-        first, second = edge_copies(index)
-
-        @pl.when(me > 0)
-        def _():
-            first.wait_send()
-
-        @pl.when(me < n - 1)
-        def _():
-            second.wait_send()
-
-    @all_peers
-    def _(k):
-        feat_copy(k).start()
-
-    edges_start(0)
-    all_feats[me] = feats[...]
-
     @pl.loop(0, D)
     def _(i):
-        acc[i] = times(three_shifts(block[i].astype(F32)), own_w[0])
+        v = with_rows(p32, own_rows, i)
+        block[i] = v.astype(BF)
+        acc[i] = times(three_shifts(v), own_w[0])
 
     @all_peers
     def _(k):
@@ -315,9 +320,9 @@
     )
     col_base[...] = col_part + jnp.concatenate([shift[1:2, :]] * 2, axis=1)
 
-    def unpacked(index, i):
-        u = edges[index, 2, i].astype(F32)
-        d = edges[index, 3, i].astype(F32)
+    def unpacked(i):
+        u = edges[2, i].astype(F32)
+        d = edges[3, i].astype(F32)
         return jnp.where(low, u, half_roll(d)), jnp.where(low, half_roll(u), d)
 
     def add_sums(sums, a):
@@ -347,17 +352,25 @@
         gain = jnp.concatenate([scale[index : index + 1, :]] * 2, axis=1)
         return average, gain * lax.rsqrt(spread + epsilon)
 
+    rows_up = rounded(all_feats[jnp.maximum(me - 1, 0)], w_row2)[D:]
+    rows_dn = rounded(all_feats[jnp.minimum(me + 1, n - 1)], w_row2)[:D]
+    halo_rows = jnp.where(low, rows_up, rows_dn)
+
     edges_wait_recv(0)
+    for h in range(halves):
+        where = slice(h * 128, h * 128 + 128)
+        h32[h, 0] = halo_up[:, :, where].astype(F32).reshape(ch * D, 128)
+        h32[h, 1] = halo_dn[:, :, where].astype(F32).reshape(ch * D, 128)
 
     def first_edge(i, sums):
         results = []
-        for offset, v in zip((0, D // 2), unpacked(0, i)):
-            v = jnp.where(inside, v, 0.0)
+        for offset in (0, D // 2):
+            v = jnp.where(inside, with_rows(h32, halo_rows, i + offset), 0.0)
             a = acc[i + offset] + times(three_shifts(v), halo_w[0]) + col_conv[...]
             acc[i + offset] = a
             sums = add_sums(sums, a)
             results.append(a)
-        pack(1, i, *results)
+        pack(i, *results)
         return sums
 
     sums = lax.fori_loop(0, D // 2, first_edge, (zeros, zeros))
@@ -374,7 +387,7 @@
     edges_wait_recv(1)
 
     def second_edge(i, sums):
-        for offset, v in zip((0, D // 2), unpacked(1, i)):
+        for offset, v in zip((0, D // 2), unpacked(i)):
             v = jnp.where(inside, elu((v - average) * factor + base), 0.0)
             a = acc[i + offset] + times(three_shifts(v), halo_w[1])
             acc[i + offset] = a
@@ -410,10 +423,10 @@
             odd = jnp.where(low, half_roll(first), second).reshape(half, 1, D, 128)
             m = jnp.concatenate([even, odd], axis=1).reshape(128, 128)
             t = (0.5 * (block[i, where, :].astype(F32) + m)).T
-            p32[which, pl.ds(i, ch, stride=rows), :] = t[:ch]
-            p32[which, pl.ds(i + D, ch, stride=rows), :] = t[ch:]
-
-        out_v[which] = p32[which].reshape(ch, rows, 128).astype(BF)
+            o32[which, pl.ds(i, ch, stride=rows), :] = t[:ch]
+            o32[which, pl.ds(i + D, ch, stride=rows), :] = t[ch:]
+
+        out_v[which] = o32[which].reshape(ch, rows, 128).astype(BF)
         copy = pltpu.make_async_copy(out_v.at[which], out.at[:, :, where], out_sem.at[which])
         copy.start()
         return copy
@@ -477,21 +490,22 @@
         out_specs=pl.BlockSpec(memory_space=pl.ANY),
         scratch_shapes=[
             *[pltpu.VMEM(a.shape, a.dtype) for a in (residue_feats,) + rest],
-            pltpu.VMEM((ch, rows, cols), BF),
-            pltpu.VMEM((halves, ch * rows, 128), F32),
+            *[pltpu.VMEM((ch, D, cols), BF)] * 4,
+            *[pltpu.VMEM((halves, 2, ch * D, 128), F32)] * 2,
             pltpu.VMEM((n,) + residue_feats.shape, BF),
             pltpu.VMEM((2, 128, 384), BF),
             pltpu.VMEM((2, 128, 384), BF),
             pltpu.VMEM((cols, 128), F32),
             pltpu.VMEM((cols, 128), F32),
             pltpu.VMEM((D, cols, 128), F32),
-            pltpu.VMEM((2, 4, D // 2, cols, 128), BF),
+            pltpu.VMEM((4, D // 2, cols, 128), BF),
             pltpu.VMEM((2, n, 8, 128), F32),
             pltpu.VMEM((D, cols, 128), BF),
             pltpu.VMEM((n, D, rows, 128), BF),
             pltpu.VMEM((n * D * rows, 128), F32),
+            pltpu.VMEM((halves, ch * rows, 128), F32),
             pltpu.VMEM((halves, ch, rows, 128), BF),
-            dma((8,)),
+            dma((9,)),
             dma((n,)), dma((n,)), dma((2, n)), dma((2, n)), dma((2, 2)), dma((2, 2)),
             dma((n,)), dma((n,)), dma((2,)),
         ],

time: 48.1 us -> 47.8 us (level)
  no operation moved by 1% of the time
where the time goes in v3:
time: 47.8 us; the launch traced here: 47.6 us
  Pallas kernels  45.8 us (96%)
  local copies, waits for them, and re-layouts  1.87 us (4%)
    pallas_call x1, Pallas kernels, fused_body(): pl.pallas_call(functools.partial(fused, n), out_shape=jax.ShapeDtypeStruc...  45.8 us
    unnamed x1, local copies, waits for them, and re-layouts  1.87 us

profile of v3, /device:TPU:0, one launch (start us, length us, event | category | flops | bytes accessed | tf_op | source)
XLA Modules:
  0.0 47.6 jit_solution(3237114364451298271)
XLA Ops:
  0.0 45.8 %shard_map.82 = bf16[64,16,256]{2,1,0:T(8,128)(2,1)} custom-call(bf16[64,16,256]{2,1,0:T(8,128)(2,1)} %pair_hbm.1, bf16[16,256]{1,0:T(8,128)(2,1)} %feats_hbm.1, bf16[64,256]{1,0:T(8,128)(2,1)} %bitcast.2, bf16[64,256]{1,0:T(8,128)(2,1)} %bitcast.3, bf16[9,64,64]{2,1,0:T(8,128)(2,1)} %taps1_hbm.1, bf16[9,64,64]{2,1,0:T(8,128)(2,1)} %taps2_hbm.1, ...), custom_call_target="tpu_custom_call" | custom-call | tf_op jit(solution)/shard_map/pallas_call | solution.py:486
  45.8 1.9 %copy.10 = bf16[64,16,256]{2,1,0:T(8,128)(2,1)} copy(bf16[64,16,256]{2,1,0:T(8,128)(2,1)} %shard_map.82) | data formatting | bytes 1048576

commit v4 on v3

--- a/solution.py
+++ b/solution.py
@@ -134,7 +134,7 @@
     out,
     feats, w_row, w_col, taps1, taps2, scale, shift,
     pair_up, pair_dn, halo_up, halo_dn, p32, h32, all_feats, own_w, halo_w, col_conv, col_base, acc,
-    edges, stats, block, mirror, m32, o32, out_v,
+    edges, stats, block, tiles, mirror, m32, o32, out_v,
     in_sem, feat_s, feat_r, stat_s, stat_r, edge_s, edge_r, mir_s, mir_r, out_sem,
 ):
     me = lax.axis_index("gx")
@@ -201,10 +201,7 @@
 
     def mirror_copy(k):
         peer = peer_of(k)
-        start = pl.multiple_of(peer * rows, rows)
-        return copy_to(
-            block.at[:, pl.ds(start, rows), :], mirror.at[me], mir_s.at[k], mir_r.at[k], peer
-        )
+        return copy_to(tiles.at[peer], mirror.at[me], mir_s.at[k], mir_r.at[k], peer)
 
     def edge_copies(index):
         above, below = jnp.maximum(me - 1, 0), jnp.minimum(me + 1, n - 1)
@@ -303,7 +300,7 @@
             bottom = jnp.concatenate([none, t[6 + kx]], axis=1)
             halo_w[index, :, where] = jnp.concatenate([top, bottom], axis=0).astype(BF)
 
-    @pl.loop(0, D)
+    @pl.loop(0, D, unroll=D)
     def _(i):
         v = with_rows(p32, own_rows, i)
         block[i] = v.astype(BF)
@@ -373,13 +370,13 @@
         pack(i, *results)
         return sums
 
-    sums = lax.fori_loop(0, D // 2, first_edge, (zeros, zeros))
+    sums = lax.fori_loop(0, D // 2, first_edge, (zeros, zeros), unroll=D // 2)
     publish(0, sums)
     edges_start(1)
     average, factor = collect(0)
     base = jnp.concatenate([shift[0:1, :]] * 2, axis=1)
 
-    @pl.loop(0, D)
+    @pl.loop(0, D, unroll=D)
     def _(i):
         a = elu((acc[i] - average) * factor + base)
         acc[i] = times(three_shifts(a), own_w[1])
@@ -394,18 +391,18 @@
             sums = add_sums(sums, a)
         return sums
 
-    sums = lax.fori_loop(0, D // 2, second_edge, (zeros, zeros))
+    sums = lax.fori_loop(0, D // 2, second_edge, (zeros, zeros), unroll=D // 2)
     publish(1, sums)
     average2, factor2 = collect(1)
 
     def result_of(which):
         where = pl.ds(pl.multiple_of(which * 128, 128), 128)
 
-        @pl.loop(0, D)
+        @pl.loop(0, D, unroll=D)
         def _(i):
             v = block[i, where, :].astype(F32) + col_base[where, :]
             v = v + (acc[i, where, :] - average2) * factor2
-            block[i, where, :] = elu(v).astype(BF)
+            tiles[pl.ds(which * half, half), i] = elu(v).astype(BF).reshape(half, rows, 128)
 
     def widen(e):
         start = pl.multiple_of(e * (D * rows), D * rows)
@@ -415,14 +412,15 @@
         where = pl.ds(pl.multiple_of(which * 128, 128), 128)
         offset = which * (half * D * rows)
 
-        @pl.loop(0, D)
+        @pl.loop(0, D, unroll=D)
         def _(i):
             first = m32[pl.ds(offset + i, half * D, stride=rows), :]
             second = m32[pl.ds(offset + i + D, half * D, stride=rows), :]
             even = jnp.where(low, first, half_roll(second)).reshape(half, 1, D, 128)
             odd = jnp.where(low, half_roll(first), second).reshape(half, 1, D, 128)
             m = jnp.concatenate([even, odd], axis=1).reshape(128, 128)
-            t = (0.5 * (block[i, where, :].astype(F32) + m)).T
+            own = tiles[pl.ds(which * half, half), i].astype(F32).reshape(128, 128)
+            t = (0.5 * (own + m)).T
             o32[which, pl.ds(i, ch, stride=rows), :] = t[:ch]
             o32[which, pl.ds(i + D, ch, stride=rows), :] = t[ch:]
 
@@ -443,7 +441,7 @@
     def _(k):
         mirror_copy(k).start()
 
-    mirror[me] = block[:, pl.ds(pl.multiple_of(me * rows, rows), rows), :]
+    mirror[me] = tiles[me]
     widen(me)
 
     @near_peers
@@ -501,7 +499,7 @@
             pltpu.VMEM((4, D // 2, cols, 128), BF),
             pltpu.VMEM((2, n, 8, 128), F32),
             pltpu.VMEM((D, cols, 128), BF),
-            pltpu.VMEM((n, D, rows, 128), BF),
+            *[pltpu.VMEM((n, D, rows, 128), BF)] * 2,
             pltpu.VMEM((n * D * rows, 128), F32),
             pltpu.VMEM((halves, ch * rows, 128), F32),
             pltpu.VMEM((halves, ch, rows, 128), BF),

time: 47.8 us -> 45.2 us (0.946)
  Pallas kernels: 45.8 us -> 43.1 us
    pallas_call x1, Pallas kernels: 45.8 us -> 43.1 us  [fused_body(): pl.pallas_call(functools.partial(fused, n), out_shape=jax.ShapeDtypeStruc...]
where the time goes in v4:
time: 45.2 us; the launch traced here: 45 us
  Pallas kernels  43.1 us (95%)
  local copies, waits for them, and re-layouts  1.87 us (4%)
    pallas_call x1, Pallas kernels, fused_body(): pl.pallas_call(functools.partial(fused, n), out_shape=jax.ShapeDtypeStruc...  43.1 us
    unnamed x1, local copies, waits for them, and re-layouts  1.87 us

profile of v4, /device:TPU:0, one launch (start us, length us, event | category | flops | bytes accessed | tf_op | source)
XLA Modules:
  0.0 45.0 jit_solution(12581757944905944708)
XLA Ops:
  0.0 43.1 %shard_map.82 = bf16[64,16,256]{2,1,0:T(8,128)(2,1)} custom-call(bf16[64,16,256]{2,1,0:T(8,128)(2,1)} %pair_hbm.1, bf16[16,256]{1,0:T(8,128)(2,1)} %feats_hbm.1, bf16[64,256]{1,0:T(8,128)(2,1)} %bitcast.2, bf16[64,256]{1,0:T(8,128)(2,1)} %bitcast.3, bf16[9,64,64]{2,1,0:T(8,128)(2,1)} %taps1_hbm.1, bf16[9,64,64]{2,1,0:T(8,128)(2,1)} %taps2_hbm.1, ...), custom_call_target="tpu_custom_call" | custom-call | tf_op jit(solution)/shard_map/pallas_call | solution.py:484
  43.1 1.9 %copy.10 = bf16[64,16,256]{2,1,0:T(8,128)(2,1)} copy(bf16[64,16,256]{2,1,0:T(8,128)(2,1)} %shard_map.82) | data formatting | bytes 1048576

commit v5 on v4

--- a/solution.py
+++ b/solution.py
@@ -133,7 +133,7 @@
     pair_hbm, feats_hbm, w_row_hbm, w_col_hbm, taps1_hbm, taps2_hbm, scale_hbm, shift_hbm,
     out,
     feats, w_row, w_col, taps1, taps2, scale, shift,
-    pair_up, pair_dn, halo_up, halo_dn, p32, h32, all_feats, own_w, halo_w, col_conv, col_base, acc,
+    pair_up, pair_dn, halo_up, halo_dn, p32, h32, parts_own, parts_all, own_w, halo_w, col_conv, col_base, acc,
     edges, stats, block, tiles, mirror, m32, o32, out_v,
     in_sem, feat_s, feat_r, stat_s, stat_r, edge_s, edge_r, mir_s, mir_r, out_sem,
 ):
@@ -180,8 +180,17 @@
     ]
     for load in loads:
         load.start()
-    for load in loads[:3]:
+    for load in loads[:5]:
         load.wait()
+
+    def packed_rows(w):
+        both = times(feats[...], jnp.concatenate([w[...]] * 2, axis=0))
+        return jnp.where(low, both[:D], both[D:]).astype(BF)
+
+    packed = jnp.concatenate([packed_rows(w_col), packed_rows(w_row)], axis=0)
+    own_rows = packed[D:].astype(F32)
+    parts_own[...] = packed
+    parts_all[me] = packed
     pl.semaphore_wait(barrier, n - 1)
 
     def copy_to(src, dst, s, r, peer):
@@ -191,7 +200,7 @@
         )
 
     def feat_copy(k):
-        return copy_to(feats, all_feats.at[me], feat_s.at[k], feat_r.at[k], peer_of(k))
+        return copy_to(parts_own, parts_all.at[me], feat_s.at[k], feat_r.at[k], peer_of(k))
 
     def stat_copy(index, k):
         return copy_to(
@@ -254,18 +263,10 @@
         feat_copy(k).start()
 
     edges_start(0)
-    all_feats[me] = feats[...]
-
-    for load in loads[3:]:
+
+    for load in loads[5:]:
         load.wait()
 
-    def rounded(a, w):
-        return times(a, w).astype(BF).astype(F32)
-
-    w_row2 = jnp.concatenate([w_row[...]] * 2, axis=0)
-    w_col2 = jnp.concatenate([w_col[...]] * 2, axis=0)
-    own_rows = rounded(feats[...], w_row2)
-    own_rows = jnp.where(low, own_rows[:D], own_rows[D:])
     halves = cols // 128
     for h in range(halves):
         where = slice(h * 128, h * 128 + 128)
@@ -311,7 +312,11 @@
         feat_copy(k).wait_recv()
 
     inside = jnp.where(low, (me > 0).astype(F32), (me < n - 1).astype(F32)) > 0.5
-    col_part = rounded(all_feats[...].reshape(n * rows, feats.shape[1]), w_col2)
+    part = parts_all[...].astype(F32)[:, :D].reshape(n * D, 128)
+    swapped = half_roll(part)
+    even = jnp.where(low, part, swapped).reshape(n, 1, D, 128)
+    odd = jnp.where(low, swapped, part).reshape(n, 1, D, 128)
+    col_part = jnp.concatenate([even, odd], axis=1).reshape(cols, 128)
     col_conv[...] = times(three_shifts(col_part), own_w[0]) + times(
         three_shifts(jnp.where(inside, col_part, 0.0)), halo_w[0]
     )
@@ -332,7 +337,7 @@
         for v in sums:
             v = jnp.sum(v, axis=0, keepdims=True)
             lines.append(v + half_roll(v))
-        stats[index, me] = jnp.concatenate(lines + [jnp.zeros((6, 128), F32)], axis=0)
+        stats[index, me] = jnp.where(low, lines[0], lines[1])
 
         @all_peers
         def _(k):
@@ -344,14 +349,15 @@
             stat_copy(index, k).wait_recv()
 
         total = jnp.sum(stats[index], axis=0)
-        average = total[0:1] / cells
-        spread = total[1:2] / cells - average * average
+        swapped = half_roll(total)
+        average = jnp.where(low, total, swapped) / cells
+        spread = jnp.where(low, swapped, total) / cells - average * average
         gain = jnp.concatenate([scale[index : index + 1, :]] * 2, axis=1)
         return average, gain * lax.rsqrt(spread + epsilon)
 
-    rows_up = rounded(all_feats[jnp.maximum(me - 1, 0)], w_row2)[D:]
-    rows_dn = rounded(all_feats[jnp.minimum(me + 1, n - 1)], w_row2)[:D]
-    halo_rows = jnp.where(low, rows_up, rows_dn)
+    rows_up = parts_all[jnp.maximum(me - 1, 0)].astype(F32)[D:]
+    rows_dn = parts_all[jnp.minimum(me + 1, n - 1)].astype(F32)[D:]
+    halo_rows = half_roll(jnp.where(low, rows_dn, rows_up))
 
     edges_wait_recv(0)
     for h in range(halves):
@@ -490,14 +496,15 @@
             *[pltpu.VMEM(a.shape, a.dtype) for a in (residue_feats,) + rest],
             *[pltpu.VMEM((ch, D, cols), BF)] * 4,
             *[pltpu.VMEM((halves, 2, ch * D, 128), F32)] * 2,
-            pltpu.VMEM((n,) + residue_feats.shape, BF),
+            pltpu.VMEM((rows, 128), BF),
+            pltpu.VMEM((n, rows, 128), BF),
             pltpu.VMEM((2, 128, 384), BF),
             pltpu.VMEM((2, 128, 384), BF),
             pltpu.VMEM((cols, 128), F32),
             pltpu.VMEM((cols, 128), F32),
             pltpu.VMEM((D, cols, 128), F32),
             pltpu.VMEM((4, D // 2, cols, 128), BF),
-            pltpu.VMEM((2, n, 8, 128), F32),
+            pltpu.VMEM((2, n, 1, 128), F32),
             pltpu.VMEM((D, cols, 128), BF),
             *[pltpu.VMEM((n, D, rows, 128), BF)] * 2,
             pltpu.VMEM((n * D * rows, 128), F32),

time: 45.2 us -> 43.3 us (0.958)
  Pallas kernels: 43.1 us -> 41.2 us
    pallas_call x1, Pallas kernels: 43.1 us -> 41.2 us  [fused_body(): pl.pallas_call(functools.partial(fused, n), out_shape=jax.ShapeDtypeStruc...]
where the time goes in v5:
time: 43.3 us; the launch traced here: 43.1 us
  Pallas kernels  41.2 us (95%)
  local copies, waits for them, and re-layouts  1.87 us (4%)
    pallas_call x1, Pallas kernels, fused_body(): pl.pallas_call(functools.partial(fused, n), out_shape=jax.ShapeDtypeStruc...  41.2 us
    unnamed x1, local copies, waits for them, and re-layouts  1.87 us

profile of v5, /device:TPU:0, one launch (start us, length us, event | category | flops | bytes accessed | tf_op | source)
XLA Modules:
  0.0 43.1 jit_solution(18064533820571925228)
XLA Ops:
  0.0 41.2 %shard_map.82 = bf16[64,16,256]{2,1,0:T(8,128)(2,1)} custom-call(bf16[64,16,256]{2,1,0:T(8,128)(2,1)} %pair_hbm.1, bf16[16,256]{1,0:T(8,128)(2,1)} %feats_hbm.1, bf16[64,256]{1,0:T(8,128)(2,1)} %bitcast.2, bf16[64,256]{1,0:T(8,128)(2,1)} %bitcast.3, bf16[9,64,64]{2,1,0:T(8,128)(2,1)} %taps1_hbm.1, bf16[9,64,64]{2,1,0:T(8,128)(2,1)} %taps2_hbm.1, ...), custom_call_target="tpu_custom_call" | custom-call | tf_op jit(solution)/shard_map/pallas_call | solution.py:490
  41.2 1.9 %copy.10 = bf16[64,16,256]{2,1,0:T(8,128)(2,1)} copy(bf16[64,16,256]{2,1,0:T(8,128)(2,1)} %shard_map.82) | data formatting | bytes 1048576
